TPU v7x, 32 devices: a whole 2x2x4 slice. The times are simulated.
32 devices in a mesh: delay: 4 (over y, core), row: 8 (over z, x).
Axes of the slice: x: 2, y: 2, z: 4, core: 2. Of those that a mesh axis runs over, the one named last changes fastest.
Arguments:
- incident: bfloat16 [64, 4096], P(None, 'row'), may hold values from -12 to 12
- onset: int32 [64], replicated, may hold values from 0 to 2
- beta: float32 [4096], P('delay'), may hold values from 0.05 to 0.5
- inverse_block: bfloat16 [4096, 4096], P('row', 'delay'), may hold values from -0.0625 to 0.0625
- delay_blocks: bfloat16 [4, 4096, 4096], P('delay', None, 'row'), may hold values from -0.09375 to 0.09375
- history_sum: float32 [4, 64, 4096], P('delay', None, 'row'), may hold values from -12 to 12
Outputs:
- currents: bfloat16 [3, 64, 4096], P(None, None, 'delay')
- carried: float32 [4, 64, 4096], P('delay', None, 'row')
All inputs are finite; a program needn't handle non-finite values.
Results may differ from a plain program's by a relative error of at most 0.0056.
Values may be sent and summed in bfloat16 or wider, within the bound.
No kernel may reach another device: no remote copies, remote signals or barrier semaphores. Data moves between devices by JAX's collectives and lax.ppermute only.
A program may use at most 64 MiB of HBM per device.

v0:
```python
import jax
import jax.numpy as jnp
from jax import lax
from jax.sharding import PartitionSpec as P

STEPS = 3


def broadcast(value, axis, source):
    kept = jnp.where(lax.axis_index(axis) == source, value, 0).astype(value.dtype)
    return lax.psum(kept, axis)


def passed_along(value, axis, by):
    devices = lax.axis_size(axis)
    pairs = [(i, i + by) for i in range(devices) if 0 <= i + by < devices]
    return lax.ppermute(value, axis, pairs)


def per_device(incident, onset, beta, inverse_block, delay_blocks, history_sum):
    future = history_sum[0]
    matrix = delay_blocks[0]
    incident_wide = incident.astype(jnp.float32)
    outputs = []
    for step_index in range(STEPS):
        offset_time = (step_index - onset).astype(jnp.float32)
        envelope = jnp.where(offset_time >= 0.0, jnp.exp(-((offset_time - 1.0) ** 2) / 4.0), 0.0)
        residual = (incident_wide * envelope[:, None] - future).astype(jnp.bfloat16)
        residual = broadcast(residual, "delay", 0)
        partial_sum = jnp.dot(residual, inverse_block, preferred_element_type=jnp.float32)
        solved = lax.psum(partial_sum, "row")
        current = (solved / (1.0 + beta[None, :] * solved * solved)).astype(jnp.bfloat16)
        gathered = lax.all_gather(current, "delay", axis=1, tiled=True)
        outputs.append(current)
        passed = passed_along(future, "delay", -1)
        future = passed + jnp.dot(gathered, matrix, preferred_element_type=jnp.float32)
    return (jnp.stack(outputs), future[None])


def solution(mesh):
    placed = (
        P(None, "row"),
        P(),
        P("delay"),
        P("row", "delay"),
        P("delay", None, "row"),
        P("delay", None, "row"),
    )
    return jax.shard_map(
        per_device,
        mesh=mesh,
        in_specs=placed,
        out_specs=(P(None, None, "delay"), P("delay", None, "row")),
        check_vma=False,
    )
```

profile of v0, /device:TPU:0, one launch (start us, length us, event | category | flops | bytes accessed | tf_op | source)
XLA Modules:
  0.0 373.9 jit_solution(11729659785771976091)
XLA Ops:
  7.2 0.7 compare_select_fusion.1
  8.0 1.7 fusion.26
  9.7 35.4 %all-reduce.7.cloned.1.call-done = bf16[64,512]{1,0:T(8,128)(2,1)} async-done(((bf16[64,512]{1,0:T(8,128)(2,1)}), bf16[64,512]{1,0:T(8,128)(2,1)}) %all-reduce.7.cloned.1.call-update) | async-done | bytes 65552 | tf_op jit(solution)/shard_map/psum | solution.py:11
  45.2 1.8 fusion.27
  47.1 1.3 collective-permute-start
  48.4 71.8 %all-reduce.9.cloned.1.call-done = f32[64,1024]{1,0:T(8,128)} async-done(((f32[64,1024]{1,0:T(8,128)}), f32[64,1024]{1,0:T(8,128)}) %all-reduce.9.cloned.1.call-update) | async-done | bytes 262160 | tf_op jit(solution)/shard_map/psum | solution.py:31
  120.2 1.0 fusion.17
  121.2 7.2 %all_gather.9 = bf16[64,4096]{1,0:T(8,128)(2,1)S(1)} all-gather(bf16[64,1024]{1,0:T(8,128)(2,1)S(1)} %fusion.17), channel_id=1, replica_groups=mesh['delay'=4,'row'=8] {'delay'}, dimensions={1}, use_global_device_ids=true | all-gather | bytes 655360 | tf_op jit(solution)/shard_map/all_gather | solution.py:33
  128.3 3.7 fusion.25
  132.1 30.2 %all-reduce.11.cloned.1.call-done = bf16[64,512]{1,0:T(8,128)(2,1)} async-done(((bf16[64,512]{1,0:T(8,128)(2,1)}), bf16[64,512]{1,0:T(8,128)(2,1)}) %all-reduce.11.cloned.1.call-update) | async-done | bytes 65552 | tf_op jit(solution)/shard_map/psum | solution.py:11
  162.3 1.8 fusion.28
  164.2 1.3 collective-permute-start.1
  165.5 71.6 %all-reduce.13.cloned.1.call-done = f32[64,1024]{1,0:T(8,128)} async-done(((f32[64,1024]{1,0:T(8,128)}), f32[64,1024]{1,0:T(8,128)}) %all-reduce.13.cloned.1.call-update) | async-done | bytes 262160 | tf_op jit(solution)/shard_map/psum | solution.py:31
  237.1 1.1 fusion.16
  238.2 7.2 %all_gather.10 = bf16[64,4096]{1,0:T(8,128)(2,1)S(1)} all-gather(bf16[64,1024]{1,0:T(8,128)(2,1)S(1)} %fusion.16), channel_id=1, replica_groups=mesh['delay'=4,'row'=8] {'delay'}, dimensions={1}, use_global_device_ids=true | all-gather | bytes 655360 | tf_op jit(solution)/shard_map/all_gather | solution.py:33
  245.3 3.0 fusion.2
  249.2 30.2 %all-reduce.15.cloned.1.call-done = bf16[64,512]{1,0:T(8,128)(2,1)} async-done(((bf16[64,512]{1,0:T(8,128)(2,1)}), bf16[64,512]{1,0:T(8,128)(2,1)}) %all-reduce.15.cloned.1.call-update) | async-done | bytes 65552 | tf_op jit(solution)/shard_map/psum | solution.py:11
  279.4 1.8 fusion.29
  281.3 1.3 collective-permute-start.2
  282.7 71.5 %all-reduce.17.cloned.1.call-done = f32[64,1024]{1,0:T(8,128)} async-done(((f32[64,1024]{1,0:T(8,128)}), f32[64,1024]{1,0:T(8,128)}) %all-reduce.17.cloned.1.call-update) | async-done | bytes 262160 | tf_op jit(solution)/shard_map/psum | solution.py:31
  354.2 1.1 fusion.15
  355.3 7.2 %all_gather.11 = bf16[64,4096]{1,0:T(8,128)(2,1)S(1)} all-gather(bf16[64,1024]{1,0:T(8,128)(2,1)S(1)} %fusion.15), channel_id=1, replica_groups=mesh['delay'=4,'row'=8] {'delay'}, dimensions={1}, use_global_device_ids=true | all-gather | bytes 655360 | tf_op jit(solution)/shard_map/all_gather | solution.py:33
  362.4 3.0 fusion
  365.5 0.8 pad_maximum_fusion
  (32 shorter events, 1.9 us)
Async XLA Ops:
  7.2 38.0 %copy-start = (bf16[512,1024]{1,0:T(8,128)(2,1)S(1)}, bf16[512,1024]{1,0:T(8,128)(2,1)}, u32[]{:S(2)}) copy-start(bf16[512,1024]{1,0:T(8,128)(2,1)} %param.9) | copy-start | bytes 3145732
  7.2 38.0 %all-reduce.7.cloned.1.call-start = ((), (), s32[]{:S(2)}) async-start(), calls=%async_computation | async-start | bytes 131072 | tf_op jit(solution)/shard_map/psum | solution.py:11
  9.7 110.5 %all-reduce.9.cloned.1.call-start = ((), (), s32[]{:S(2)}) async-start(), calls=%async_computation.1 | async-start | bytes 524288 | tf_op jit(solution)/shard_map/psum | solution.py:31
  47.0 190.1 %copy-start.5 = (f32[1024]{0:T(1024)S(1)}, f32[1024]{0:T(1024)}, u32[]{:S(2)}) copy-start(f32[1024]{0:T(1024)} %param.8) | copy-start | bytes 12292
  47.0 115.2 %all-reduce.11.cloned.1.call-start = ((), (), s32[]{:S(2)}) async-start(), calls=%async_computation.2 | async-start | bytes 131072 | tf_op jit(solution)/shard_map/psum | solution.py:11
  47.1 81.2 %collective-permute-start = (f32[64,512]{1,0:T(8,128)}, f32[64,512]{1,0:T(8,128)S(1)}, u32[]{:S(2)}, u32[]{:S(2)}) collective-permute-start(f32[64,512]{1,0:T(8,128)} %bitcast.30), channel_id=1, source_target_pairs={{8,0},{16,8},{24,16},{9,1},{17,9},{25,17},{10,2},{18,10},{26,18},{... | collective-permute-start | bytes 393224 | tf_op jit(solution)/shard_map/ppermute | solution.py:17
  132.0 116.4 %copy-start.4 = (bf16[64,512]{1,0:T(8,128)(2,1)S(1)}, bf16[64,512]{1,0:T(8,128)(2,1)}, u32[]{:S(2)}) copy-start(bf16[64,512]{1,0:T(8,128)(2,1)} %param.6) | copy-start | bytes 196612
  132.0 105.1 %all-reduce.13.cloned.1.call-start = ((), (), s32[]{:S(2)}) async-start(), calls=%async_computation.3 | async-start | bytes 524288 | tf_op jit(solution)/shard_map/psum | solution.py:31
  164.1 117.1 %copy-start.1 = (f32[64,1024]{1,0:T(8,128)S(1)}, f32[64,1024]{1,0:T(8,128)}, u32[]{:S(2)}) copy-start(f32[64,1024]{1,0:T(8,128)} %all-reduce.9.cloned.1.call-done) | copy-start | bytes 786436
  164.1 115.2 %all-reduce.15.cloned.1.call-start = ((), (), s32[]{:S(2)}) async-start(), calls=%async_computation.4 | async-start | bytes 131072 | tf_op jit(solution)/shard_map/psum | solution.py:11
  164.2 84.2 %collective-permute-start.1 = (f32[64,512]{1,0:T(8,128)S(1)}, f32[64,512]{1,0:T(8,128)S(1)}, u32[]{:S(2)}, u32[]{:S(2)}) collective-permute-start(f32[64,512]{1,0:T(8,128)S(1)} %get-tuple-element.8), channel_id=1, source_target_pairs={{8,0},{16,8},{24,16},{9,1},{17,9},{25,17},{10,2},{18,10},{26,18},{... | collective-permute-start | bytes 393224 | tf_op jit(solution)/shard_map/ppermute | solution.py:17
  237.1 45.5 %copy-start.2 = (f32[64,1024]{1,0:T(8,128)S(1)}, f32[64,1024]{1,0:T(8,128)}, u32[]{:S(2)}) copy-start(f32[64,1024]{1,0:T(8,128)} %all-reduce.13.cloned.1.call-done) | copy-start | bytes 786436
  249.1 105.1 %all-reduce.17.cloned.1.call-start = ((), (), s32[]{:S(2)}) async-start(), calls=%async_computation.5 | async-start | bytes 524288 | tf_op jit(solution)/shard_map/psum | solution.py:31
  281.3 85.0 %collective-permute-start.2 = (f32[64,512]{1,0:T(8,128)S(1)}, f32[64,512]{1,0:T(8,128)S(1)}, u32[]{:S(2)}, u32[]{:S(2)}) collective-permute-start(f32[64,512]{1,0:T(8,128)S(1)} %get-tuple-element.3), channel_id=1, source_target_pairs={{8,0},{16,8},{24,16},{9,1},{17,9},{25,17},{10,2},{18,10},{26,18},{... | collective-permute-start | bytes 393224 | tf_op jit(solution)/shard_map/ppermute | solution.py:17
  354.2 11.3 %copy-start.3 = (f32[64,1024]{1,0:T(8,128)S(1)}, f32[64,1024]{1,0:T(8,128)}, u32[]{:S(2)}) copy-start(f32[64,1024]{1,0:T(8,128)} %all-reduce.17.cloned.1.call-done) | copy-start | bytes 786436
Sparse Core Ops, SparseCore 0:
  10.9 34.2 all-reduce.6
  49.1 71.0 all-reduce.8
  132.1 30.0 all-reduce.10
  166.0 71.0 all-reduce.12
  249.3 30.0 all-reduce.14
  283.1 71.0 all-reduce.16
where the time goes:
time: 374 us
  waiting for transfers between devices  311 us (83%)
  blocking collectives  21.5 us (6%)
  matrix products  15.2 us (4%)
  between operations  14.2 us (4%)
  other arithmetic  7.92 us (2%)
  starting transfers between devices  4.12 us (1%)
    psum x3, waiting for transfers between devices, per_device(): solved = lax.psum(partial_sum, 'row')  215 us
    psum x3, waiting for transfers between devices, broadcast(): return lax.psum(kept, axis)  95.8 us
    all_gather x3, blocking collectives, per_device(): gathered = lax.all_gather(current, 'delay', axis=1, tiled=True)  21.5 us
    dot_general x3, matrix products, per_device(): jnp.dot(gathered, matrix, preferred_element_type=jnp.float32)  9.7 us
  transfers between devices with their start and end apart: 9, of which 6 were waited for; matrix products, arithmetic and copies ran while one was open for 3% of the time, Pallas kernels for 0%

commit v1 on v0

--- a/solution.py
+++ b/solution.py
@@ -28,7 +28,7 @@
         residual = (incident_wide * envelope[:, None] - future).astype(jnp.bfloat16)
         residual = broadcast(residual, "delay", 0)
         partial_sum = jnp.dot(residual, inverse_block, preferred_element_type=jnp.float32)
-        solved = lax.psum(partial_sum, "row")
+        solved = jnp.sum(lax.all_gather(partial_sum, "row"), axis=0)
         current = (solved / (1.0 + beta[None, :] * solved * solved)).astype(jnp.bfloat16)
         gathered = lax.all_gather(current, "delay", axis=1, tiled=True)
         outputs.append(current)

time: 374 us -> 306 us (0.82)
  waiting for transfers between devices: 311 us -> 240 us
    psum x3 -> x0, waiting for transfers between devices: 215 us -> none  [per_device(): solved = lax.psum(partial_sum, 'row')]
    all_gather x0 -> x3, waiting for transfers between devices: none -> 146 us  [per_device(): solved = jnp.sum(lax.all_gather(partial_sum, 'row'), axis=0)]
    reduce_sum x0 -> x3, other arithmetic: none -> 5.25 us  [per_device(): solved = jnp.sum(lax.all_gather(partial_sum, 'row'), axis=0)]
  transfers between devices with their start and end apart: 9 -> 9, of which waited for: 6 -> 6; matrix products, arithmetic and copies ran while one was open for 3% -> 4% of each run, Pallas kernels for 0% -> 0%
where the time goes in v1:
time: 306 us; the launch traced here: 305 us
  waiting for transfers between devices  240 us (78%)
  blocking collectives  21.4 us (7%)
  matrix products  15.2 us (5%)
  between operations  14.2 us (5%)
  other arithmetic  10.2 us (3%)
  starting transfers between devices  4.12 us (1%)
    all_gather x3, waiting for transfers between devices, per_device(): solved = jnp.sum(lax.all_gather(partial_sum, 'row'), axis=0)  146 us
    psum x3, waiting for transfers between devices, broadcast(): return lax.psum(kept, axis)  94.5 us
    all_gather x3, blocking collectives, per_device(): gathered = lax.all_gather(current, 'delay', axis=1, tiled=True)  21.4 us
    dot_general x3, matrix products, per_device(): jnp.dot(gathered, matrix, preferred_element_type=jnp.float32)  9.7 us
  transfers between devices with their start and end apart: 9, of which 6 were waited for; matrix products, arithmetic and copies ran while one was open for 4% of the time, Pallas kernels for 0%

profile of v1, /device:TPU:0, one launch (start us, length us, event | category | flops | bytes accessed | tf_op | source)
XLA Modules:
  0.0 305.4 jit_solution(5191150774690111473)
XLA Ops:
  7.3 0.7 compare_select_fusion.1
  8.0 1.7 fusion.35
  9.7 35.4 %all-reduce.4.cloned.1.call-done = bf16[64,512]{1,0:T(8,128)(2,1)} async-done(((bf16[64,512]{1,0:T(8,128)(2,1)}), bf16[64,512]{1,0:T(8,128)(2,1)}) %all-reduce.4.cloned.1.call-update) | async-done | bytes 65552 | tf_op jit(solution)/shard_map/psum | solution.py:11
  45.2 1.8 fusion.36
  47.1 1.3 collective-permute-start
  48.4 48.6 %all-gather.7.cloned.1.call-done = f32[512,1024]{1,0:T(8,128)} async-done(((f32[64,1024]{1,0:T(8,128)}), f32[512,1024]{1,0:T(8,128)}) %all-gather.7.cloned.1.call-update) | async-done | bytes 2097168 | tf_op jit(solution)/shard_map/all_gather | solution.py:31
  97.0 1.7 reduce_sum.33
  98.8 7.1 %all_gather.29 = bf16[64,4096]{1,0:T(8,128)(2,1)S(1)} all-gather(bf16[64,1024]{1,0:T(8,128)(2,1)S(1)} %fusion.25), channel_id=1, replica_groups=mesh['delay'=4,'row'=8] {'delay'}, dimensions={1}, use_global_device_ids=true | all-gather | bytes 655360 | tf_op jit(solution)/shard_map/all_gather | solution.py:33
  106.0 3.7 %fusion.34 = (bf16[64,512]{1,0:T(8,128)(2,1)}, f32[64,512]{1,0:T(8,128)S(1)}) fusion(bf16[64,512]{1,0:T(8,128)(2,1)S(1)} %copy-done.1, f32[64]{0:T(128)S(1)} %get-tuple-element.7, pred[]{:T(512)S(6)} %eq.2, f32[64,512]{1,0:T(8,128)S(1)} %collective-permute-done, bf16[64,4096]{1,0:T(8,128)(2,1)S(1)} %all_gather.29, bf16[1,4096,512]{2,1,0:T(8,128)(2,1)} %param.10), kind=kOutput, calls=%fused_computation.43 | convolution fusion | flops 268632064 | bytes 5112065 | tf_op jit(solution)/shard_map/dot_general | solution.py:36
  109.7 29.5 %all-reduce.6.cloned.1.call-done = bf16[64,512]{1,0:T(8,128)(2,1)} async-done(((bf16[64,512]{1,0:T(8,128)(2,1)}), bf16[64,512]{1,0:T(8,128)(2,1)}) %all-reduce.6.cloned.1.call-update) | async-done | bytes 65552 | tf_op jit(solution)/shard_map/psum | solution.py:11
  139.2 1.8 fusion.37
  141.2 1.3 collective-permute-start.1
  142.5 48.5 %all-gather.9.cloned.1.call-done = f32[512,1024]{1,0:T(8,128)} async-done(((f32[64,1024]{1,0:T(8,128)}), f32[512,1024]{1,0:T(8,128)}) %all-gather.9.cloned.1.call-update) | async-done | bytes 2097168 | tf_op jit(solution)/shard_map/all_gather | solution.py:31
  190.9 1.7 reduce_sum.35
  192.7 7.1 %all_gather.32 = bf16[64,4096]{1,0:T(8,128)(2,1)S(1)} all-gather(bf16[64,1024]{1,0:T(8,128)(2,1)S(1)} %fusion.23), channel_id=1, replica_groups=mesh['delay'=4,'row'=8] {'delay'}, dimensions={1}, use_global_device_ids=true | all-gather | bytes 655360 | tf_op jit(solution)/shard_map/all_gather | solution.py:33
  199.9 3.0 fusion.2
  203.7 29.5 %all-reduce.8.cloned.1.call-done = bf16[64,512]{1,0:T(8,128)(2,1)} async-done(((bf16[64,512]{1,0:T(8,128)(2,1)}), bf16[64,512]{1,0:T(8,128)(2,1)}) %all-reduce.8.cloned.1.call-update) | async-done | bytes 65552 | tf_op jit(solution)/shard_map/psum | solution.py:11
  233.2 1.8 fusion.38
  235.1 1.3 collective-permute-start.2
  236.4 48.5 %all-gather.11.cloned.1.call-done = f32[512,1024]{1,0:T(8,128)} async-done(((f32[64,1024]{1,0:T(8,128)}), f32[512,1024]{1,0:T(8,128)}) %all-gather.11.cloned.1.call-update) | async-done | bytes 2097168 | tf_op jit(solution)/shard_map/all_gather | solution.py:31
  284.9 1.7 reduce_sum.37
  286.7 7.1 %all_gather.35 = bf16[64,4096]{1,0:T(8,128)(2,1)S(1)} all-gather(bf16[64,1024]{1,0:T(8,128)(2,1)S(1)} %fusion.21), channel_id=1, replica_groups=mesh['delay'=4,'row'=8] {'delay'}, dimensions={1}, use_global_device_ids=true | all-gather | bytes 655360 | tf_op jit(solution)/shard_map/all_gather | solution.py:33
  293.9 3.0 fusion
  297.1 0.8 pad_maximum_fusion
  (27 shorter events, 2.1 us)
Async XLA Ops:
  7.2 38.0 %copy-start = (bf16[512,1024]{1,0:T(8,128)(2,1)S(1)}, bf16[512,1024]{1,0:T(8,128)(2,1)}, u32[]{:S(2)}) copy-start(bf16[512,1024]{1,0:T(8,128)(2,1)} %param.9) | copy-start | bytes 3145732
  7.2 98.8 %copy-start.1 = (bf16[64,512]{1,0:T(8,128)(2,1)S(1)}, bf16[64,512]{1,0:T(8,128)(2,1)}, u32[]{:S(2)}) copy-start(bf16[64,512]{1,0:T(8,128)(2,1)} %param.6) | copy-start | bytes 196612
  7.2 91.5 %copy-start.2 = (f32[1024]{0:T(1024)S(1)}, f32[1024]{0:T(1024)}, u32[]{:S(2)}) copy-start(f32[1024]{0:T(1024)} %param.8) | copy-start | bytes 12292
  7.2 38.0 %all-reduce.4.cloned.1.call-start = ((), (), s32[]{:S(2)}) async-start(), calls=%async_computation | async-start | bytes 131072 | tf_op jit(solution)/shard_map/psum | solution.py:11
  9.7 87.3 %all-gather.7.cloned.1.call-start = ((), (), s32[]{:S(2)}) async-start(), calls=%async_computation.3 | async-start | bytes 2359296 | tf_op jit(solution)/shard_map/all_gather | solution.py:31
  47.0 92.2 %all-reduce.6.cloned.1.call-start = ((), (), s32[]{:S(2)}) async-start(), calls=%async_computation.1 | async-start | bytes 131072 | tf_op jit(solution)/shard_map/psum | solution.py:11
  47.1 58.9 %collective-permute-start = (f32[64,512]{1,0:T(8,128)}, f32[64,512]{1,0:T(8,128)S(1)}, u32[]{:S(2)}, u32[]{:S(2)}) collective-permute-start(f32[64,512]{1,0:T(8,128)} %bitcast.42), channel_id=1, source_target_pairs={{8,0},{16,8},{24,16},{9,1},{17,9},{25,17},{10,2},{18,10},{26,18},{... | collective-permute-start | bytes 393224 | tf_op jit(solution)/shard_map/ppermute | solution.py:17
  109.7 81.2 %all-gather.9.cloned.1.call-start = ((), (), s32[]{:S(2)}) async-start(), calls=%async_computation.4 | async-start | bytes 2359296 | tf_op jit(solution)/shard_map/all_gather | solution.py:31
  141.1 92.1 %all-reduce.8.cloned.1.call-start = ((), (), s32[]{:S(2)}) async-start(), calls=%async_computation.2 | async-start | bytes 131072 | tf_op jit(solution)/shard_map/psum | solution.py:11
  141.2 61.8 %collective-permute-start.1 = (f32[64,512]{1,0:T(8,128)S(1)}, f32[64,512]{1,0:T(8,128)S(1)}, u32[]{:S(2)}, u32[]{:S(2)}) collective-permute-start(f32[64,512]{1,0:T(8,128)S(1)} %get-tuple-element.11), channel_id=1, source_target_pairs={{8,0},{16,8},{24,16},{9,1},{17,9},{25,17},{10,2},{18,10},{26,18},{... | collective-permute-start | bytes 393224 | tf_op jit(solution)/shard_map/ppermute | solution.py:17
  203.7 81.2 %all-gather.11.cloned.1.call-start = ((), (), s32[]{:S(2)}) async-start(), calls=%async_computation.5 | async-start | bytes 2359296 | tf_op jit(solution)/shard_map/all_gather | solution.py:31
  235.1 62.8 %collective-permute-start.2 = (f32[64,512]{1,0:T(8,128)S(1)}, f32[64,512]{1,0:T(8,128)S(1)}, u32[]{:S(2)}, u32[]{:S(2)}) collective-permute-start(f32[64,512]{1,0:T(8,128)S(1)} %get-tuple-element.3), channel_id=1, source_target_pairs={{8,0},{16,8},{24,16},{9,1},{17,9},{25,17},{10,2},{18,10},{26,18},{... | collective-permute-start | bytes 393224 | tf_op jit(solution)/shard_map/ppermute | solution.py:17
Sparse Core Ops, SparseCore 0:
  10.9 34.2 all-reduce.3
  47.9 49.0 all-gather.6
  109.8 29.4 all-reduce.5
  141.8 49.0 all-gather.8
  203.8 29.4 all-reduce.7
  235.8 49.0 all-gather.10
